TPU v7x, 32 devices: a whole 2x2x4 slice. The times are simulated.
32 devices in a mesh: rep: 4 (over x, y), dp: 8 (over z, core).
Axes of the slice: x: 2, y: 2, z: 4, core: 2. Of those that a mesh axis runs over, the one named last changes fastest.
Arguments:
- g_w_gate: bfloat16 [32, 2, 1280, 3072], P(('rep', 'dp')), parts along dimension 0
- g_w_up: bfloat16 [32, 2, 1280, 3072], P(('rep', 'dp')), parts along dimension 0
- g_w_down: bfloat16 [32, 2, 3072, 1280], P(('rep', 'dp')), parts along dimension 0
- w_gate: bfloat16 [2, 1280, 3072], replicated
- w_up: bfloat16 [2, 1280, 3072], replicated
- w_down: bfloat16 [2, 3072, 1280], replicated
- m_w_gate: float32 [2, 1280, 3072], P(None, 'dp')
- m_w_up: float32 [2, 1280, 3072], P(None, 'dp')
- m_w_down: float32 [2, 3072, 1280], P(None, 'dp')
- v_w_gate: float32 [2, 1280, 3072], P(None, 'dp')
- v_w_up: float32 [2, 1280, 3072], P(None, 'dp')
- v_w_down: float32 [2, 3072, 1280], P(None, 'dp')
Outputs:
- output 1: bfloat16 [8, 1280, 3072], P('rep'), parts along dimension 0
- output 2: bfloat16 [8, 1280, 3072], P('rep'), parts along dimension 0
- output 3: bfloat16 [8, 3072, 1280], P('rep'), parts along dimension 0
- output 4: float32 [8, 1280, 3072], P('rep', 'dp'), parts along dimension 0
- output 5: float32 [8, 1280, 3072], P('rep', 'dp'), parts along dimension 0
- output 6: float32 [8, 3072, 1280], P('rep', 'dp'), parts along dimension 0
- output 7: float32 [8, 1280, 3072], P('rep', 'dp'), parts along dimension 0
- output 8: float32 [8, 1280, 3072], P('rep', 'dp'), parts along dimension 0
- output 9: float32 [8, 3072, 1280], P('rep', 'dp'), parts along dimension 0
There are 4 independent parts. A program takes and returns all parts, laid end to end along the dimension named above; an argument that names none is the same for every part.
All inputs are finite; a program needn't handle non-finite values.
Results may differ from a plain program's by a relative error of at most 0.022.
Values are sent between devices in bfloat16 or wider.
A program may use at most 2 GiB of HBM per device.

v0:
```python
import jax
import jax.numpy as jnp
from jax import lax
from jax.sharding import PartitionSpec as P


def adamw(w, m, v, g):
    m = 0.9 * m + 0.1 * g
    v = 0.95 * v + 0.05 * g * g
    step = m * lax.rsqrt(v + 1e-8) + 0.1 * w
    return (w - 0.02 * step).astype(jnp.bfloat16), m, v


def clipped(gradients, sum_of_squares, count):
    factor = jnp.minimum(1.0, 0.5 * lax.rsqrt(sum_of_squares / count + 1e-30))
    return [g * factor for g in gradients]


def solution(mesh):
    def step(*arrays):
        terms, weights, m, v = (arrays[i : i + 3] for i in (0, 3, 6, 9))
        gradients = [lax.psum_scatter(t[0], "dp", scatter_dimension=1, tiled=True).astype(jnp.float32) for t in terms]
        squares = lax.psum(sum(jnp.sum(g * g) for g in gradients), "dp")
        gradients = clipped(gradients, squares, lax.psum(1, "dp") * sum(g.size for g in gradients))
        me = lax.axis_index("dp")
        own = [lax.dynamic_slice_in_dim(w, me * one.shape[1], one.shape[1], 1).astype(jnp.float32) for w, one in zip(weights, m, strict=True)]
        new = [adamw(w, m, v, g) for w, m, v, g in zip(own, m, v, gradients, strict=True)]
        whole = [lax.all_gather(one[0], "dp", axis=1, tiled=True) for one in new]
        return (*whole, *(one[1] for one in new), *(one[2] for one in new))

    all_of, cut = P(None, None, None), P(None, "dp", None)
    return jax.shard_map(
        step,
        mesh=mesh,
        in_specs=(P(("rep", "dp"), None, None, None),) * 3 + (all_of,) * 3 + (cut,) * 6,
        out_specs=(P("rep", None, None),) * 3 + (P("rep", "dp", None),) * 6,
        check_vma=False,
    )
```

profile of v0, /device:TPU:0, one launch (start us, length us, event | category | flops | bytes accessed | tf_op | source)
XLA Modules:
  0.0 983.8 jit_solution(14803456211566112487)
XLA Ops:
  7.2 0.0 reduce-scatter.4.cloned.1.call-start
  7.2 0.7 reduce-scatter.4.cloned.1.call-update
  7.9 0.0 reduce-scatter.6.cloned.1.call-start
  8.0 0.7 reduce-scatter.6.cloned.1.call-update
  8.7 0.0 reduce-scatter.8.cloned.1.call-start
  8.7 0.7 reduce-scatter.8.cloned.1.call-update
  9.4 0.0 all-gather.8.cloned.1.call-start
  9.4 162.3 %reduce-scatter.4.cloned.1.call-done = bf16[2,160,3072]{2,1,0:T(8,128)(2,1)} async-done(((bf16[2,1280,3072]{2,1,0:T(8,128)(2,1)}), bf16[2,160,3072]{2,1,0:T(8,128)(2,1)}) %reduce-scatter.4.cloned.1.call-update) | async-done | bytes 1966096 | tf_op jit(solution)/shard_map/reduce_scatter | solution.py:22
  171.7 3.2 fusion.9
  174.9 156.5 %reduce-scatter.6.cloned.1.call-done = bf16[2,160,3072]{2,1,0:T(8,128)(2,1)} async-done(((bf16[2,1280,3072]{2,1,0:T(8,128)(2,1)}), bf16[2,160,3072]{2,1,0:T(8,128)(2,1)}) %reduce-scatter.6.cloned.1.call-update) | async-done | bytes 1966096 | tf_op jit(solution)/shard_map/reduce_scatter | solution.py:22
  331.4 3.2 fusion.10
  335.9 155.2 %reduce-scatter.8.cloned.1.call-done = bf16[2,384,1280]{2,1,0:T(8,128)(2,1)} async-done(((bf16[2,3072,1280]{2,1,0:T(8,128)(2,1)}), bf16[2,384,1280]{2,1,0:T(8,128)(2,1)}) %reduce-scatter.8.cloned.1.call-update) | async-done | bytes 1966096 | tf_op jit(solution)/shard_map/reduce_scatter | solution.py:22
  491.1 3.2 fusion.11
  494.9 14.3 %psum.7 = f32[]{:T(128)} all-reduce(f32[]{:T(128)S(6)} %add.65), channel_id=1, replica_groups=mesh['rep'=4,'dp'=8] {'dp'}, use_global_device_ids=true, to_apply=%region_6.0 | all-reduce | flops 1 | bytes 8 | tf_op jit(solution)/shard_map/psum | solution.py:23
  510.0 7.8 fusion.17
  517.8 0.0 all-gather.8.cloned.1.call-update
  517.8 0.0 all-gather.4.cloned.1.call-start
  517.8 0.0 copy-start.1
  517.8 7.9 fusion.8
  525.7 0.0 all-gather.4.cloned.1.call-update
  525.7 0.0 all-gather.6.cloned.1.call-start
  525.8 0.0 copy-done.1
  525.8 6.8 fusion.14
  532.6 0.0 all-gather.6.cloned.1.call-update
  532.6 126.0 %all-gather.8.cloned.1.call-done = bf16[2,3072,1280]{2,1,0:T(8,128)(2,1)} async-done(((bf16[2,384,1280]{2,1,0:T(8,128)(2,1)}), bf16[2,3072,1280]{2,1,0:T(8,128)(2,1)}) %all-gather.8.cloned.1.call-update) | async-done | bytes 15728656 | tf_op jit(solution)/shard_map/all_gather | solution.py:28
  658.6 143.1 %all-gather.4.cloned.1.call-done = bf16[2,1280,3072]{2,1,0:T(8,128)(2,1)} async-done(((bf16[2,160,3072]{2,1,0:T(8,128)(2,1)}), bf16[2,1280,3072]{2,1,0:T(8,128)(2,1)}) %all-gather.4.cloned.1.call-update) | async-done | bytes 15728656 | tf_op jit(solution)/shard_map/all_gather | solution.py:28
  801.7 143.1 %all-gather.6.cloned.1.call-done = bf16[2,1280,3072]{2,1,0:T(8,128)(2,1)} async-done(((bf16[2,160,3072]{2,1,0:T(8,128)(2,1)}), bf16[2,1280,3072]{2,1,0:T(8,128)(2,1)}) %all-gather.6.cloned.1.call-update) | async-done | bytes 15728656 | tf_op jit(solution)/shard_map/all_gather | solution.py:28
  944.8 0.0 copy-start
  944.8 0.0 slice-start
  944.8 0.0 slice-start.1
  944.8 15.9 %copy.24 = bf16[2,1280,3072]{2,1,0:T(8,128)(2,1)} copy(bf16[2,1280,3072]{2,1,0:T(8,128)(2,1)} %all-gather.4.cloned.1.call-done) | data formatting | bytes 31457280
  960.7 0.0 copy-done
  960.7 0.0 slice-start.2
  960.7 0.0 slice-start.3
  960.7 8.0 copy.25
  968.7 0.0 slice-done
  968.7 0.0 slice-done.1
  968.7 1.5 slice-done.2
  970.2 0.9 slice-done.3
  971.1 5.8 copy.26
  (1 shorter events, 0.0 us)
Async XLA Ops:
  7.2 164.6 %reduce-scatter.4.cloned.1.call-start = ((), (), s32[]{:S(2)}) async-start(), calls=%async_computation.3 | async-start | bytes 17694720 | tf_op jit(solution)/shard_map/reduce_scatter | solution.py:22
  7.9 323.5 %reduce-scatter.6.cloned.1.call-start = ((), (), s32[]{:S(2)}) async-start(), calls=%async_computation.4 | async-start | bytes 17694720 | tf_op jit(solution)/shard_map/reduce_scatter | solution.py:22
  8.7 482.5 %reduce-scatter.8.cloned.1.call-start = ((), (), s32[]{:S(2)}) async-start(), calls=%async_computation.5 | async-start | bytes 17694720 | tf_op jit(solution)/shard_map/reduce_scatter | solution.py:22
  9.4 649.2 %all-gather.8.cloned.1.call-start = ((), (), s32[]{:S(2)}) async-start(), calls=%async_computation.8 | async-start | bytes 17694720 | tf_op jit(solution)/shard_map/all_gather | solution.py:28
  517.8 283.9 %all-gather.4.cloned.1.call-start = ((), (), s32[]{:S(2)}) async-start(), calls=%async_computation.6 | async-start | bytes 17694720 | tf_op jit(solution)/shard_map/all_gather | solution.py:28
  517.8 8.0 copy-start.1
  525.7 419.1 %all-gather.6.cloned.1.call-start = ((), (), s32[]{:S(2)}) async-start(), calls=%async_computation.7 | async-start | bytes 17694720 | tf_op jit(solution)/shard_map/all_gather | solution.py:28
  944.8 15.9 %copy-start = (bf16[2,1280,3072]{2,1,0:T(8,128)(2,1)S(1)}, bf16[2,1280,3072]{2,1,0:T(8,128)(2,1)}, u32[]{:S(2)}) copy-start(bf16[2,1280,3072]{2,1,0:T(8,128)(2,1)} %all-gather.6.cloned.1.call-done) | copy-start | bytes 47185924
  944.8 23.8 %slice-start = ((s8[15728640]{0:T(1024)(128)(4,1)}), s8[4194304]{0:T(1024)(128)(4,1)S(1)}, s32[]{:S(2)}) async-start(s8[15728640]{0:T(1024)(128)(4,1)} %bitcast.6), calls=%async_computation.9 | async-start | bytes 8388608
  944.8 23.8 %slice-start.1 = ((s8[15728640]{0:T(1024)(128)(4,1)}), s8[4194304]{0:T(1024)(128)(4,1)S(1)}, s32[]{:S(2)}) async-start(s8[15728640]{0:T(1024)(128)(4,1)} %bitcast.6), calls=%async_computation.10 | async-start | bytes 8388608
  960.7 9.5 slice-start.2
  960.7 10.4 %slice-start.3 = ((s8[15728640]{0:T(1024)(128)(4,1)}), s8[3145728]{0:T(1024)(128)(4,1)S(1)}, s32[]{:S(2)}) async-start(s8[15728640]{0:T(1024)(128)(4,1)} %bitcast.6), calls=%async_computation.12 | async-start | bytes 6291456
Sparse Core Ops, SparseCore 0:
  10.3 161.4 reduce-scatter.3
  174.0 157.3 reduce-scatter.5
  333.7 157.3 reduce-scatter.7
  517.9 140.6 all-gather.7
  660.6 141.0 all-gather.3
  803.7 141.0 all-gather.5
where the time goes:
time: 984 us
  waiting for transfers between devices  888 us (90%)
  local copies, waits for them, and re-layouts  32.1 us (3%)
  other arithmetic  31.9 us (3%)
  between operations  16.8 us (2%)
  blocking collectives  14.3 us (1%)
    reduce_scatter x3, waiting for transfers between devices, step(): lax.psum_scatter(t[0], 'dp', scatter_dimension=1, tiled=True)  474 us
    all_gather x3, waiting for transfers between devices, step(): whole = [lax.all_gather(one[0], 'dp', axis=1, tiled=True) for one in new]  412 us
    unnamed x15, local copies, waits for them, and re-layouts  32.1 us
    convert_element_type x3, other arithmetic, adamw(): return ((w - 0.02 * step).astype(jnp.bfloat16), m, v)  22.5 us
  transfers between devices with their start and end apart: 6, of which 6 were waited for; matrix products, arithmetic and copies ran while one was open for 2% of the time, Pallas kernels for 0%

commit v1 on v0

v1 whole, which is shorter than its diff:
```python
import jax
import jax.numpy as jnp
from jax import lax
from jax.experimental import pallas as pl
from jax.experimental.pallas import tpu as pltpu
from jax.sharding import PartitionSpec as P

MESH = pl.DeviceIdType.MESH
CHIPS = 4
LAYERS = 2
RS_ROWS = (16, 16, 32)
AG_ROWS = (16, 16, 32)
LAG = 2
AHEAD = 3
READ = 2


def kernel(count, *refs):
    g, w, m, v = (refs[i : i + 3] for i in (0, 3, 6, 9))
    new_w, new_m, new_v = (refs[i : i + 3] for i in (12, 15, 18))
    (land_0, land_1, land_2, peer_0, peer_1, peer_2, own_a, own_b, m_a, m_b, v_a, v_b, w_a, w_b, mo_a, mo_b, vo_a, vo_b) = refs[21:39]
    (squares_a, squares_b, part, norms) = refs[39:43]
    (own_sem, peer_send, peer_recv, sum_send, sum_recv, norm_send, norm_recv, tile_sem, out_sem, g_recv, e_recv, i_recv, f_recv, o_recv) = refs[43:57]
    (send_sem, core_send, core_recv, local_sem) = refs[57:]
    land, peer = (land_0, land_1, land_2), (peer_0, peer_1, peer_2)
    own, m_in, v_in, w_in = (own_a, own_a, own_b), (m_a, m_a, m_b), (v_a, v_a, v_b), (w_a, w_a, w_b)
    m_out, v_out, squares = (mo_a, mo_a, mo_b), (vo_a, vo_a, vo_b), (squares_a, squares_a, squares_b)
    block = [ref.shape[1] for ref in land]
    f32 = jnp.float32

    me = lax.axis_index("dp")
    z, c = lax.div(me, 2), lax.rem(me, 2)
    is_end = (z == 0) | (z == 3)
    is_inner = jnp.logical_not(is_end)
    centre = jnp.where(z == 0, 1, jnp.where(z == 3, 2, 3 - z))
    outer = jnp.where(z <= 1, 0, 3)

    def core(chip):
        return {"dp": chip * 2 + c}

    other_core = {"dp": z * 2 + 1 - c}

    def remote(src, dst, send, recv, device):
        return pltpu.make_async_remote_copy(src_ref=src, dst_ref=dst, send_sem=send, recv_sem=recv, device_id=device, device_id_type=MESH)

    barrier = pltpu.get_barrier_semaphore()
    for d in range(1, 8):
        pl.semaphore_signal(barrier, inc=1, device_id={"dp": lax.rem(me + d, 8)}, device_id_type=MESH)
    pl.semaphore_wait(barrier, 7)

    def unit_of(j, layer, chip):
        return layer * CHIPS + chip

    def push_terms(j, layer, chip):
        u = unit_of(j, layer, chip)
        rows = pl.ds(pl.multiple_of((chip * 2 + 1 - c) * block[j], block[j]), block[j])
        return remote(g[j].at[layer, rows], peer[j].at[u], peer_send.at[j], peer_recv.at[j * 8 + u], other_core)

    for j in range(3):
        for layer in range(LAYERS):
            for o in range(2):
                push_terms(j, layer, o).start()
                push_terms(j, layer, 2 + o).start()

    rs_n = [block[j] // RS_ROWS[j] for j in range(3)]
    rs_k = [LAYERS * 2 * n for n in rs_n]
    rs_total = sum(rs_k)
    ag_n = [block[j] // AG_ROWS[j] for j in range(3)]
    ag_k = [LAYERS * n for n in ag_n]
    ag_total = sum(ag_k)

    def each(counts, k, body):
        first = 0
        for j in range(3):
            last = first + counts[j]

            @pl.when((k >= first) & (k < last))
            def _(j=j, first=first):
                body(j, k - first)

            first = last

    def rs_piece(flow, j, k):
        unit, s = lax.div(k, rs_n[j]), lax.rem(k, rs_n[j])
        layer, chip = lax.div(unit, 2), lax.rem(unit, 2) + 2 * flow
        return layer, chip, s

    def rows_of(j, device, s, n):
        return pl.ds(pl.multiple_of(device * block[j] + s * n, n), n)

    def load_terms(flow, j, k, slot):
        layer, chip, s = rs_piece(flow, j, k)
        rows = rows_of(j, chip * 2 + c, s, RS_ROWS[j])
        return pltpu.make_async_copy(g[j].at[layer, rows], own[j].at[flow, slot], own_sem.at[flow, slot])

    for ref in (squares_a, squares_b):
        ref[...] = jnp.zeros_like(ref)

    def sum_step(flow, i):
        source, sink = (3, 0) if flow == 0 else (0, 3)
        lag = (3 - z if flow == 0 else z) * LAG
        to = z - 1 if flow == 0 else z + 1
        k = i - lag
        each(rs_k, k + AHEAD, lambda j, q: load_terms(flow, j, q, lax.rem(k + AHEAD, AHEAD + 1)).start())

        def body(j, q):
            layer, chip, s = rs_piece(flow, j, q)
            u, n, slot = unit_of(j, layer, chip), RS_ROWS[j], lax.rem(k, AHEAD + 1)
            rows = pl.ds(pl.multiple_of(s * n, n), n)
            here = land[j].at[u, rows]
            load_terms(flow, j, q, slot).wait()

            @pl.when(s == 0)
            def _():
                remote(peer[j].at[u], peer[j].at[u], peer_send.at[j], peer_recv.at[j * 8 + u], other_core).wait_recv()

            copy = remote(here, here, sum_send.at[flow, j], sum_recv.at[flow, k], core(jnp.clip(to, 0, 3)))

            @pl.when(z != source)
            def _():
                copy.wait_recv()

            def add(fed, last):
                for r in range(0, n, 16):
                    at = pl.ds(pl.multiple_of(s * n + r, 16), 16)
                    total = own[j][flow, slot, pl.ds(r, 16)].astype(f32) + peer[j][u, at].astype(f32)
                    if fed:
                        total = land[j][u, at].astype(f32) + total
                    total = total.astype(jnp.bfloat16)
                    land[j][u, at] = total
                    if last:
                        total = total.astype(f32)
                        total = total * total
                        squares[j][...] += total[:8] + total[8:]

            @pl.when(z == source)
            def _():
                add(False, False)

            @pl.when((z != source) & (z != sink))
            def _():
                add(True, False)

            @pl.when(z == sink)
            def _():
                add(True, True)

            @pl.when(z != sink)
            def _():
                copy.start()

        each(rs_k, k, body)

    def both(i, carry):
        sum_step(0, i - AHEAD)
        sum_step(1, i - AHEAD)
        return carry

    def ag_piece(j, k):
        layer, s = lax.div(k, ag_n[j]), lax.rem(k, ag_n[j])
        return layer, s

    def tiles(j, k, slot):
        layer, s = ag_piece(j, k)
        n = AG_ROWS[j]
        rows = pl.ds(pl.multiple_of(s * n, n), n)
        return (
            pltpu.make_async_copy(m[j].at[layer, rows], m_in[j].at[slot], tile_sem.at[0, slot]),
            pltpu.make_async_copy(v[j].at[layer, rows], v_in[j].at[slot], tile_sem.at[1, slot]),
            pltpu.make_async_copy(w[j].at[layer, rows_of(j, me, s, n)], w_in[j].at[slot], tile_sem.at[2, slot]),
        )

    def start_tiles(k):
        def body(j, q):
            for copy in tiles(j, q, lax.rem(k, READ + 1)):
                copy.start()

        each(ag_k, k, body)

    for k in range(READ):
        for copy in tiles(0, k, k):
            copy.start()

    lax.fori_loop(0, rs_total + AHEAD + 3 * LAG, both, 0)

    place = jnp.where(z == 0, c, 2 + c)

    def norm_copy(d):
        return remote(part, norms.at[place], norm_send.at[d - 1], norm_recv.at[place], {"dp": lax.rem(me + d, 8)})

    @pl.when(is_end)
    def _():
        total = jnp.sum(squares_a[...]) + jnp.sum(squares_b[...])
        part[...] = jnp.full(part.shape, total, f32)
        norms[place] = jnp.full(part.shape, total, f32)
        for d in range(1, 8):
            norm_copy(d).start()

    for p in range(4):

        @pl.when(is_inner | (place != p))
        def _():
            remote(part, norms.at[p], norm_send.at[0], norm_recv.at[p], other_core).wait_recv()

    total = norms[0] + norms[1] + norms[2] + norms[3]
    factor = jnp.minimum(1.0, 0.5 * lax.rsqrt(total / count + 1e-30))[:1, :1]

    def new_piece(j, k, chip):
        layer, s = ag_piece(j, k)
        return new_w[j].at[layer, rows_of(j, chip * 2 + c, s, AG_ROWS[j])]

    def share(j, ref):
        remote(ref, ref, core_send.at[j], core_recv.at[j], other_core).start()

    def moments_out(j, k, slot):
        layer, s = ag_piece(j, k)
        n = AG_ROWS[j]
        rows = pl.ds(pl.multiple_of(s * n, n), n)
        return (
            pltpu.make_async_copy(m_out[j].at[slot], new_m[j].at[layer, rows], out_sem.at[0, slot]),
            pltpu.make_async_copy(v_out[j].at[slot], new_v[j].at[layer, rows], out_sem.at[1, slot]),
        )

    def wait_moments(k):
        def body(j, q):
            for copy in moments_out(j, q, lax.rem(k, 2)):
                copy.wait()

        each(ag_k, k, body)

    def own_step(k):
        def body(j, q):
            start_tiles(k + READ)
            wait_moments(k - 2)
            layer, s = ag_piece(j, q)
            n, slot, out = AG_ROWS[j], lax.rem(k, READ + 1), lax.rem(k, 2)
            rows = pl.ds(pl.multiple_of(s * n, n), n)
            u_own, u_new = unit_of(j, layer, z), unit_of(j, layer, lax.bitwise_xor(z, 1))
            u_handed = unit_of(j, layer, centre)

            @pl.when(is_end)
            def _():
                remote(land[j].at[u_handed, rows], peer[j].at[u_handed, rows], send_sem.at[0, j], g_recv.at[k], core(centre)).start()

            for copy in tiles(j, q, slot):
                copy.wait()

            @pl.when(is_inner)
            def _():
                remote(land[j].at[u_own, rows], peer[j].at[u_own, rows], send_sem.at[0, j], g_recv.at[k], core(centre)).wait_recv()

            def update(sums):
                for r in range(0, n, 16):
                    at, tile = pl.ds(pl.multiple_of(s * n + r, 16), 16), pl.ds(r, 16)
                    clipped = sums[j][u_own, at].astype(f32) * factor
                    one_m = 0.9 * m_in[j][slot, tile] + 0.1 * clipped
                    one_v = 0.95 * v_in[j][slot, tile] + 0.05 * clipped * clipped
                    one_w = w_in[j][slot, tile].astype(f32)
                    step = one_m * lax.rsqrt(one_v + 1e-8) + 0.1 * one_w
                    m_out[j][out, tile] = one_m
                    v_out[j][out, tile] = one_v
                    peer[j][u_new, at] = (one_w - 0.02 * step).astype(jnp.bfloat16)

            @pl.when(is_end)
            def _():
                update(land)

            @pl.when(is_inner)
            def _():
                update(peer)

            for copy in moments_out(j, q, out):
                copy.start()
            ready, there = peer[j].at[u_new, rows], new_piece(j, q, z)

            @pl.when(is_end)
            def _():
                remote(ready, there, send_sem.at[1, j], e_recv.at[k], core(centre)).start()

            @pl.when(is_inner)
            def _():
                remote(ready, there, send_sem.at[0, j], i_recv.at[k], core(outer)).start()
                remote(ready, there, send_sem.at[1, j], i_recv.at[k], core(centre)).start()

            remote(ready, there, core_send.at[j], core_recv.at[j], other_core).start()
            pltpu.make_async_copy(ready, there, local_sem.at[j]).start()

        each(ag_k, k, body)

    def arrived(k, chip, recv, forward=None):
        def body(j, q):
            ref = new_piece(j, q, chip)
            remote(ref, ref, core_send.at[j], recv.at[k], other_core).wait_recv()
            if forward is not None:
                sem, to = forward
                remote(ref, ref, send_sem.at[sem, j], f_recv.at[k], core(to)).start()
            share(j, ref)

        each(ag_k, k, body)

    near, far = jnp.where(z <= 1, 1, 2), 3 - outer

    def new_step(i, carry):
        @pl.when(is_end)
        def _():
            own_step(i)
            arrived(i - 2 * LAG, near, i_recv)
            arrived(i - 3 * LAG, far, f_recv)

        @pl.when(is_inner)
        def _():
            arrived(i - 2 * LAG, far, f_recv, (3, outer))
            arrived(i - LAG, outer, e_recv, (2, centre))
            own_step(i - LAG)
            arrived(i - 2 * LAG, centre, i_recv)

        return carry

    lax.fori_loop(0, ag_total + 3 * LAG, new_step, 0)

    def last_piece(j, layer, chip):
        return new_w[j].at[layer, pl.ds(pl.multiple_of((chip * 2 + c) * block[j], block[j]), block[j])]

    @pl.when(is_inner)
    def _():
        for j in range(3):
            for layer in range(LAYERS):
                ref = last_piece(j, layer, centre)
                remote(ref, ref, send_sem.at[4, j], o_recv.at[j * LAYERS + layer], core(outer)).start()

    @pl.when(is_end)
    def _():
        for j in range(3):
            for layer in range(LAYERS):
                ref = last_piece(j, layer, 3 - near)
                remote(ref, ref, core_send.at[j], o_recv.at[j * LAYERS + layer], other_core).wait_recv()
                share(j, ref)

    wait_moments(ag_total - 2)
    wait_moments(ag_total - 1)

    def wait_send(ref, sem):
        remote(ref, ref, sem, sem, other_core).wait_send()

    for j in range(3):
        half = land[j].at[pl.ds(0, 4)]
        mine = land[j].at[pl.ds(0, LAYERS)]
        wait_send(land[j], peer_send.at[j])

        @pl.when(z != 0)
        def _():
            wait_send(half, sum_send.at[0, j])

        @pl.when(z != 3)
        def _():
            wait_send(half, sum_send.at[1, j])

        wait_send(mine, send_sem.at[0, j])
        wait_send(mine, send_sem.at[1, j])

        @pl.when(is_inner)
        def _():
            for sem in (2, 3, 4):
                wait_send(mine, send_sem.at[sem, j])

        wait_send(land[j], core_send.at[j])
        remote(land[j], land[j], core_send.at[j], core_recv.at[j], other_core).wait_recv()
        pltpu.make_async_copy(mine, peer[j].at[pl.ds(0, LAYERS)], local_sem.at[j]).wait()

    @pl.when(is_end)
    def _():
        for d in range(1, 8):
            norm_copy(d).wait_send()


def solution(mesh):
    def step(*arrays):
        terms, weights, m, v = (arrays[i : i + 3] for i in (0, 3, 6, 9))
        terms = [t.reshape(t.shape[1:]) for t in terms]
        shapes = [one.shape for one in m]
        count = sum(t.size for t in terms)
        rs_total = sum(LAYERS * 2 * s[1] // r for s, r in zip(shapes, RS_ROWS, strict=True))
        ag_total = sum(LAYERS * s[1] // r for s, r in zip(shapes, AG_ROWS, strict=True))
        units = [pltpu.VMEM((LAYERS * CHIPS, s[1], s[2]), jnp.bfloat16) for s in shapes]
        wide, tall = shapes[0], shapes[2]

        def pair(slots, rows, dtype):
            return [pltpu.VMEM((*slots, rows[0], wide[2]), dtype), pltpu.VMEM((*slots, rows[2], tall[2]), dtype)]

        dma = pltpu.SemaphoreType.DMA
        outs = pl.pallas_call(
            lambda *refs: kernel(count, *refs),
            out_shape=[jax.ShapeDtypeStruct(one.shape, jnp.bfloat16) for one in weights]
            + [jax.ShapeDtypeStruct(one.shape, jnp.float32) for one in (*m, *v)],
            in_specs=[pl.BlockSpec(memory_space=pl.ANY)] * 12,
            out_specs=[pl.BlockSpec(memory_space=pl.ANY)] * 9,
            scratch_shapes=units
            + units
            + pair((2, AHEAD + 1), RS_ROWS, jnp.bfloat16)
            + pair((READ + 1,), AG_ROWS, jnp.float32)
            + pair((READ + 1,), AG_ROWS, jnp.float32)
            + pair((READ + 1,), AG_ROWS, jnp.bfloat16)
            + pair((2,), AG_ROWS, jnp.float32)
            + pair((2,), AG_ROWS, jnp.float32)
            + [pltpu.VMEM((8, wide[2]), jnp.float32), pltpu.VMEM((8, tall[2]), jnp.float32)]
            + [pltpu.VMEM((8, 128), jnp.float32), pltpu.VMEM((4, 8, 128), jnp.float32)]
            + [
                dma((2, AHEAD + 1)),
                dma((3,)),
                dma((24,)),
                dma((2, 3)),
                dma((2, rs_total)),
                dma((7,)),
                dma((4,)),
                dma((3, READ + 1)),
                dma((2, 2)),
                dma((ag_total,)),
                dma((ag_total,)),
                dma((ag_total,)),
                dma((ag_total,)),
                dma((3 * LAYERS,)),
                dma((5, 3)),
                dma((3,)),
                dma((3,)),
                dma((3,)),
            ],
            name="clipped_step",
            compiler_params=pltpu.CompilerParams(collective_id=0, has_side_effects=True, vmem_limit_bytes=67043328),
        )(*terms, *weights, *m, *v)
        return tuple(outs)

    all_of, cut = P(None, None, None), P(None, "dp", None)
    return jax.shard_map(
        step,
        mesh=mesh,
        in_specs=(P(("rep", "dp"), None, None, None),) * 3 + (all_of,) * 3 + (cut,) * 6,
        out_specs=(P("rep", None, None),) * 3 + (P("rep", "dp", None),) * 6,
        check_vma=False,
    )
```

time: 984 us -> 732 us (0.74)
  waiting for transfers between devices: 888 us -> 0 us
  Pallas kernels: 0 us -> 678 us
  other arithmetic: 31.9 us -> 0.01 us
  local copies, waits for them, and re-layouts: 32.1 us -> 52.4 us
  between operations: 16.8 us -> 0.7 us
  blocking collectives: 14.3 us -> 0 us
    pallas_call x0 -> x1, Pallas kernels: none -> 678 us  [step(): pl.pallas_call(lambda *refs: kernel(count, *refs), out_shape=[jax.ShapeDt...]
    reduce_scatter x3 -> x0, waiting for transfers between devices: 474 us -> none  [step(): lax.psum_scatter(t[0], 'dp', scatter_dimension=1, tiled=True)]
    all_gather x3 -> x0, waiting for transfers between devices: 412 us -> none  [step(): whole = [lax.all_gather(one[0], 'dp', axis=1, tiled=True) for one in new]]
    convert_element_type x3 -> x0, other arithmetic: 22.5 us -> none  [adamw(): return ((w - 0.02 * step).astype(jnp.bfloat16), m, v)]
    unnamed x15 -> x31, local copies, waits for them, and re-layouts: 32.1 us -> 52.4 us
    psum x1 -> x0, blocking collectives: 14.3 us -> none  [step(): squares = lax.psum(sum((jnp.sum(g * g) for g in gradients)), 'dp')]
  transfers between devices with their start and end apart: 6 -> 0, of which waited for: 6 -> 0; matrix products, arithmetic and copies ran while one was open for 2% -> 0% of each run, Pallas kernels for 0% -> 0%
where the time goes in v1:
time: 732 us; the launch traced here: 731 us
  Pallas kernels  678 us (93%)
  local copies, waits for them, and re-layouts  52.4 us (7%)
    pallas_call x1, Pallas kernels, step(): pl.pallas_call(lambda *refs: kernel(count, *refs), out_shape=[jax.ShapeDt...  678 us
    unnamed x31, local copies, waits for them, and re-layouts  52.4 us

profile of v1, /device:TPU:0, one launch (start us, length us, event | category | flops | bytes accessed | tf_op | source)
XLA Modules:
  0.0 731.5 jit_solution(5573238273074054942)
XLA Ops:
  0.6 678.3 %clipped_step.1 = (bf16[2,1280,3072]{2,1,0:T(8,128)(2,1)}, bf16[2,1280,3072]{2,1,0:T(8,128)(2,1)}, bf16[2,3072,1280]{2,1,0:T(8,128)(2,1)}, f32[2,160,3072]{2,1,0...) custom-call(bf16[2,1280,3072]{2,1,0:T(8,128)(2,1)} %bitcast.3, ...), custom_call_target="tpu_custom_call" | custom-call | tf_op jit(solution)/shard_map/clipped_step/pallas_call | solution.py:391
  679.0 0.0 copy-start
  679.0 0.0 slice-start
  679.0 0.0 slice-start.1
  679.0 15.9 %copy.30 = bf16[2,1280,3072]{2,1,0:T(8,128)(2,1)} copy(bf16[2,1280,3072]{2,1,0:T(8,128)(2,1)} %get-tuple-element.18) | data formatting | bytes 31457280
  694.9 0.0 copy-done
  694.9 0.0 slice-start.2
  694.9 0.0 slice-start.3
  694.9 8.0 %copy.31 = bf16[2,1280,3072]{2,1,0:T(8,128)(2,1)} copy(bf16[2,1280,3072]{2,1,0:T(8,128)(2,1)S(1)} %copy-done) | data formatting | bytes 31457280
  702.9 0.0 slice-done
  702.9 0.0 slice-done.1
  702.9 1.5 slice-done.2
  704.4 0.9 slice-done.3
  705.3 0.0 copy-start.6
  705.3 6.6 copy.32
  711.9 0.0 copy-done.6
  711.9 0.0 copy-start.5
  711.9 2.0 copy.33
  713.9 1.5 copy-done.5
  715.4 0.0 copy-start.4
  715.4 2.0 copy.34
  717.4 1.5 copy-done.4
  719.0 0.0 copy-start.3
  719.0 2.0 copy.35
  721.0 1.5 copy-done.3
  722.5 0.0 copy-start.2
  722.5 2.0 copy.36
  724.5 1.5 copy-done.2
  726.0 0.0 copy-start.1
  726.0 2.0 copy.37
  728.0 1.5 copy-done.1
  729.6 1.9 copy.38
  (1 shorter events, 0.0 us)
Async XLA Ops:
  679.0 15.9 %copy-start = (bf16[2,1280,3072]{2,1,0:T(8,128)(2,1)S(1)}, bf16[2,1280,3072]{2,1,0:T(8,128)(2,1)}, u32[]{:S(2)}) copy-start(bf16[2,1280,3072]{2,1,0:T(8,128)(2,1)} %get-tuple-element.19) | copy-start | bytes 47185924
  679.0 23.9 %slice-start = ((s8[15728640]{0:T(1024)(128)(4,1)}), s8[4194304]{0:T(1024)(128)(4,1)S(1)}, s32[]{:S(2)}) async-start(s8[15728640]{0:T(1024)(128)(4,1)} %bitcast.6), calls=%async_computation | async-start | bytes 8388608
  679.0 23.9 %slice-start.1 = ((s8[15728640]{0:T(1024)(128)(4,1)}), s8[4194304]{0:T(1024)(128)(4,1)S(1)}, s32[]{:S(2)}) async-start(s8[15728640]{0:T(1024)(128)(4,1)} %bitcast.6), calls=%async_computation.1 | async-start | bytes 8388608
  694.9 9.5 %slice-start.2 = ((s8[15728640]{0:T(1024)(128)(4,1)}), s8[4194304]{0:T(1024)(128)(4,1)S(1)}, s32[]{:S(2)}) async-start(s8[15728640]{0:T(1024)(128)(4,1)} %bitcast.6), calls=%async_computation.2 | async-start | bytes 8388608
  694.9 10.4 %slice-start.3 = ((s8[15728640]{0:T(1024)(128)(4,1)}), s8[3145728]{0:T(1024)(128)(4,1)S(1)}, s32[]{:S(2)}) async-start(s8[15728640]{0:T(1024)(128)(4,1)} %bitcast.6), calls=%async_computation.3 | async-start | bytes 6291456
  705.3 6.6 copy-start.6
  711.9 3.5 copy-start.5
  715.4 3.5 copy-start.4
  719.0 3.5 copy-start.3
  722.5 3.5 copy-start.2
  726.0 3.5 copy-start.1

commit v2 on v1

--- a/solution.py
+++ b/solution.py
@@ -5,23 +5,28 @@
 from jax.experimental.pallas import tpu as pltpu
 from jax.sharding import PartitionSpec as P
 
+
 MESH = pl.DeviceIdType.MESH
 CHIPS = 4
 LAYERS = 2
 RS_ROWS = (16, 16, 32)
 AG_ROWS = (16, 16, 32)
 LAG = 2
+SINK_LAG = 12
+NEW_LAG = 2
+HANDED = 4
 AHEAD = 3
 READ = 2
 
 
 def kernel(count, *refs):
     g, w, m, v = (refs[i : i + 3] for i in (0, 3, 6, 9))
-    new_w, new_m, new_v = (refs[i : i + 3] for i in (12, 15, 18))
+    new_w, hand, new_m, new_v = (refs[i : i + 3] for i in (12, 15, 18, 21))
+    refs = refs[3:]
     (land_0, land_1, land_2, peer_0, peer_1, peer_2, own_a, own_b, m_a, m_b, v_a, v_b, w_a, w_b, mo_a, mo_b, vo_a, vo_b) = refs[21:39]
     (squares_a, squares_b, part, norms) = refs[39:43]
-    (own_sem, peer_send, peer_recv, sum_send, sum_recv, norm_send, norm_recv, tile_sem, out_sem, g_recv, e_recv, i_recv, f_recv, o_recv) = refs[43:57]
-    (send_sem, core_send, core_recv, local_sem) = refs[57:]
+    (own_sem, peer_send, peer_recv, sum_send, sum_recv, norm_send, norm_recv, tile_sem, out_sem, g_recv, e_recv, i_recv, f_recv) = refs[43:56]
+    (send_sem, core_send, core_recv, local_sem) = refs[56:]
     land, peer = (land_0, land_1, land_2), (peer_0, peer_1, peer_2)
     own, m_in, v_in, w_in = (own_a, own_a, own_b), (m_a, m_a, m_b), (v_a, v_a, v_b), (w_a, w_a, w_b)
     m_out, v_out, squares = (mo_a, mo_a, mo_b), (vo_a, vo_a, vo_b), (squares_a, squares_a, squares_b)
@@ -48,11 +53,11 @@
         pl.semaphore_signal(barrier, inc=1, device_id={"dp": lax.rem(me + d, 8)}, device_id_type=MESH)
     pl.semaphore_wait(barrier, 7)
 
-    def unit_of(j, layer, chip):
+    def unit_of(layer, chip):
         return layer * CHIPS + chip
 
     def push_terms(j, layer, chip):
-        u = unit_of(j, layer, chip)
+        u = unit_of(layer, chip)
         rows = pl.ds(pl.multiple_of((chip * 2 + 1 - c) * block[j], block[j]), block[j])
         return remote(g[j].at[layer, rows], peer[j].at[u], peer_send.at[j], peer_recv.at[j * 8 + u], other_core)
 
@@ -98,14 +103,15 @@
 
     def sum_step(flow, i):
         source, sink = (3, 0) if flow == 0 else (0, 3)
-        lag = (3 - z if flow == 0 else z) * LAG
+        hops = 3 - z if flow == 0 else z
+        lag = jnp.where(hops == 3, SINK_LAG, jnp.where(hops == 2, LAG, 0))
         to = z - 1 if flow == 0 else z + 1
         k = i - lag
         each(rs_k, k + AHEAD, lambda j, q: load_terms(flow, j, q, lax.rem(k + AHEAD, AHEAD + 1)).start())
 
         def body(j, q):
             layer, chip, s = rs_piece(flow, j, q)
-            u, n, slot = unit_of(j, layer, chip), RS_ROWS[j], lax.rem(k, AHEAD + 1)
+            u, n, slot = unit_of(layer, chip), RS_ROWS[j], lax.rem(k, AHEAD + 1)
             rows = pl.ds(pl.multiple_of(s * n, n), n)
             here = land[j].at[u, rows]
             load_terms(flow, j, q, slot).wait()
@@ -181,7 +187,21 @@
         for copy in tiles(0, k, k):
             copy.start()
 
-    lax.fori_loop(0, rs_total + AHEAD + 3 * LAG, both, 0)
+    lax.fori_loop(0, rs_total + AHEAD + SINK_LAG, both, 0)
+
+    def hand_on(k):
+        def body(j, q):
+            layer, s = ag_piece(j, q)
+            n = AG_ROWS[j]
+            u, rows = unit_of(layer, centre), pl.ds(pl.multiple_of(s * n, n), n)
+            remote(land[j].at[u, rows], peer[j].at[u, rows], send_sem.at[0, j], g_recv.at[k], core(centre)).start()
+
+        each(ag_k, k, body)
+
+    @pl.when(is_end)
+    def _():
+        for k in range(HANDED):
+            hand_on(jnp.int32(k))
 
     place = jnp.where(z == 0, c, 2 + c)
 
@@ -209,8 +229,6 @@
         layer, s = ag_piece(j, k)
         return new_w[j].at[layer, rows_of(j, chip * 2 + c, s, AG_ROWS[j])]
 
-    def share(j, ref):
-        remote(ref, ref, core_send.at[j], core_recv.at[j], other_core).start()
 
     def moments_out(j, k, slot):
         layer, s = ag_piece(j, k)
@@ -235,12 +253,7 @@
             layer, s = ag_piece(j, q)
             n, slot, out = AG_ROWS[j], lax.rem(k, READ + 1), lax.rem(k, 2)
             rows = pl.ds(pl.multiple_of(s * n, n), n)
-            u_own, u_new = unit_of(j, layer, z), unit_of(j, layer, lax.bitwise_xor(z, 1))
-            u_handed = unit_of(j, layer, centre)
-
-            @pl.when(is_end)
-            def _():
-                remote(land[j].at[u_handed, rows], peer[j].at[u_handed, rows], send_sem.at[0, j], g_recv.at[k], core(centre)).start()
+            u_own, u_new = unit_of(layer, z), unit_of(layer, lax.bitwise_xor(z, 1))
 
             for copy in tiles(j, q, slot):
                 copy.wait()
@@ -276,25 +289,29 @@
             @pl.when(is_end)
             def _():
                 remote(ready, there, send_sem.at[1, j], e_recv.at[k], core(centre)).start()
+                hand_on(k + HANDED)
 
             @pl.when(is_inner)
             def _():
                 remote(ready, there, send_sem.at[0, j], i_recv.at[k], core(outer)).start()
-                remote(ready, there, send_sem.at[1, j], i_recv.at[k], core(centre)).start()
+                remote(ready, hand[j].at[layer, rows], send_sem.at[1, j], i_recv.at[k], core(centre)).start()
 
             remote(ready, there, core_send.at[j], core_recv.at[j], other_core).start()
             pltpu.make_async_copy(ready, there, local_sem.at[j]).start()
 
         each(ag_k, k, body)
 
-    def arrived(k, chip, recv, forward=None):
+    def arrived(k, chip, recv, forward=None, handed=False):
         def body(j, q):
-            ref = new_piece(j, q, chip)
+            ref = there = new_piece(j, q, chip)
+            if handed:
+                layer, s = ag_piece(j, q)
+                ref = hand[j].at[layer, pl.ds(pl.multiple_of(s * AG_ROWS[j], AG_ROWS[j]), AG_ROWS[j])]
             remote(ref, ref, core_send.at[j], recv.at[k], other_core).wait_recv()
             if forward is not None:
                 sem, to = forward
                 remote(ref, ref, send_sem.at[sem, j], f_recv.at[k], core(to)).start()
-            share(j, ref)
+            remote(ref, there, core_send.at[j], core_recv.at[j], other_core).start()
 
         each(ag_k, k, body)
 
@@ -304,37 +321,19 @@
         @pl.when(is_end)
         def _():
             own_step(i)
-            arrived(i - 2 * LAG, near, i_recv)
-            arrived(i - 3 * LAG, far, f_recv)
+            arrived(i - NEW_LAG, near, i_recv)
+            arrived(i - 3 * NEW_LAG, far, f_recv)
 
         @pl.when(is_inner)
         def _():
-            arrived(i - 2 * LAG, far, f_recv, (3, outer))
-            arrived(i - LAG, outer, e_recv, (2, centre))
-            own_step(i - LAG)
-            arrived(i - 2 * LAG, centre, i_recv)
+            own_step(i)
+            arrived(i - 2 * NEW_LAG, far, f_recv, (3, outer))
+            arrived(i - NEW_LAG, outer, e_recv, (2, centre))
+            arrived(i - NEW_LAG, centre, i_recv, handed=True)
 
         return carry
 
-    lax.fori_loop(0, ag_total + 3 * LAG, new_step, 0)
-
-    def last_piece(j, layer, chip):
-        return new_w[j].at[layer, pl.ds(pl.multiple_of((chip * 2 + c) * block[j], block[j]), block[j])]
-
-    @pl.when(is_inner)
-    def _():
-        for j in range(3):
-            for layer in range(LAYERS):
-                ref = last_piece(j, layer, centre)
-                remote(ref, ref, send_sem.at[4, j], o_recv.at[j * LAYERS + layer], core(outer)).start()
-
-    @pl.when(is_end)
-    def _():
-        for j in range(3):
-            for layer in range(LAYERS):
-                ref = last_piece(j, layer, 3 - near)
-                remote(ref, ref, core_send.at[j], o_recv.at[j * LAYERS + layer], other_core).wait_recv()
-                share(j, ref)
+    lax.fori_loop(0, ag_total + 3 * NEW_LAG, new_step, 0)
 
     wait_moments(ag_total - 2)
     wait_moments(ag_total - 1)
@@ -360,17 +359,110 @@
 
         @pl.when(is_inner)
         def _():
-            for sem in (2, 3, 4):
+            for sem in (2, 3):
                 wait_send(mine, send_sem.at[sem, j])
 
-        wait_send(land[j], core_send.at[j])
-        remote(land[j], land[j], core_send.at[j], core_recv.at[j], other_core).wait_recv()
+        def wait_core(ref):
+            wait_send(ref, core_send.at[j])
+            remote(ref, ref, core_send.at[j], core_recv.at[j], other_core).wait_recv()
+
+        @pl.when(is_end)
+        def _():
+            wait_core(land[j].at[pl.ds(0, 3 * LAYERS)])
+
+        @pl.when(is_inner)
+        def _():
+            wait_core(land[j])
+
         pltpu.make_async_copy(mine, peer[j].at[pl.ds(0, LAYERS)], local_sem.at[j]).wait()
 
     @pl.when(is_end)
     def _():
         for d in range(1, 8):
             norm_copy(d).wait_send()
+
+
+def settle(parts, *refs):
+    w, hand, rest, results = refs[:3], refs[3:6], refs[6:12], refs[12:21]
+    slots, (in_sem, out_sem) = refs[21:25], refs[25:]
+    me = lax.axis_index("dp")
+    z, c = lax.div(me, 2), lax.rem(me, 2)
+    is_inner = (z == 1) | (z == 2)
+    items, used = [], [0] * 4
+
+    def item(pool, src, dst, other=None, chosen=None):
+        items.append((pool, used[pool] % slots[pool].shape[0], src, dst, other, chosen))
+        used[pool] += 1
+
+    for j in range(3):
+        rows = w[j].shape[1] // (2 * CHIPS)
+        for layer in range(LAYERS):
+            for d in range(2 * CHIPS):
+                at = (layer, pl.ds(d * rows, rows))
+                item(j // 2, w[j].at[at], results[j].at[at], hand[j].at[layer], is_inner & (d == (3 - z) * 2 + c))
+    for i in range(6):
+        for layer in range(LAYERS):
+            item(2 + i % 3 // 2, rest[i].at[layer], results[3 + i].at[layer])
+
+    def get(t, src):
+        pool, slot = items[t][:2]
+        return pltpu.make_async_copy(src, slots[pool].at[slot], in_sem.at[pool, slot])
+
+    def put(t):
+        pool, slot, _, dst = items[t][:4]
+        return pltpu.make_async_copy(slots[pool].at[slot], dst, out_sem.at[pool, slot])
+
+    busy = {}
+    for t in range(len(items) + parts):
+        if t < len(items):
+            pool, slot, src, _, other, chosen = items[t]
+            if (pool, slot) in busy:
+                put(busy.pop((pool, slot))).wait()
+            if other is None:
+                get(t, src).start()
+            else:
+
+                @pl.when(chosen)
+                def _():
+                    get(t, other).start()
+
+                @pl.when(jnp.logical_not(chosen))
+                def _():
+                    get(t, src).start()
+
+        if t >= parts:
+            done = t - parts
+            get(done, items[done][2]).wait()
+            put(done).start()
+            busy[items[done][:2]] = done
+    for t in busy.values():
+        put(t).wait()
+
+
+def place(n, *refs):
+    mine, others, results, buffers = (refs[i * n : (i + 1) * n] for i in (1, 2, 3, 4))
+    in_sem, out_sem = refs[5 * n :]
+    me = lax.axis_index("dp")
+    z, c = lax.div(me, 2), lax.rem(me, 2)
+
+    @pl.when((z == 0) | (z == 3))
+    def _():
+        chip = jnp.where(z == 0, 2, 1)
+        gets, puts = [], []
+        for j in range(n):
+            rows = mine[j].shape[1]
+            for b, (src, core) in enumerate(((mine[j], c), (others[j], 1 - c))):
+                for layer in range(LAYERS):
+                    at = pl.ds(pl.multiple_of((chip * 2 + core) * rows, rows), rows)
+                    gets.append(pltpu.make_async_copy(src.at[layer], buffers[j].at[b, layer], in_sem.at[j, b, layer]))
+                    puts.append(pltpu.make_async_copy(buffers[j].at[b, layer], results[j].at[layer, at], out_sem.at[j, b, layer]))
+        for copy in gets:
+            copy.start()
+        for get, put in zip(gets, puts, strict=True):
+            get.wait()
+            put.start()
+        for copy in puts:
+            copy.wait()
 
 
 def solution(mesh):
@@ -391,9 +483,10 @@
         outs = pl.pallas_call(
             lambda *refs: kernel(count, *refs),
             out_shape=[jax.ShapeDtypeStruct(one.shape, jnp.bfloat16) for one in weights]
+            + [jax.ShapeDtypeStruct(one.shape, jnp.bfloat16) for one in m]
             + [jax.ShapeDtypeStruct(one.shape, jnp.float32) for one in (*m, *v)],
             in_specs=[pl.BlockSpec(memory_space=pl.ANY)] * 12,
-            out_specs=[pl.BlockSpec(memory_space=pl.ANY)] * 9,
+            out_specs=[pl.BlockSpec(memory_space=pl.ANY)] * 12,
             scratch_shapes=units
             + units
             + pair((2, AHEAD + 1), RS_ROWS, jnp.bfloat16)
@@ -418,8 +511,7 @@
                 dma((ag_total,)),
                 dma((ag_total,)),
                 dma((ag_total,)),
-                dma((3 * LAYERS,)),
-                dma((5, 3)),
+                dma((4, 3)),
                 dma((3,)),
                 dma((3,)),
                 dma((3,)),
@@ -427,7 +519,49 @@
             name="clipped_step",
             compiler_params=pltpu.CompilerParams(collective_id=0, has_side_effects=True, vmem_limit_bytes=67043328),
         )(*terms, *weights, *m, *v)
-        return tuple(outs)
+        whole, hand, rest = outs[:3], outs[3:6], outs[6:]
+        came = []
+        for one in hand:
+            came.append(lax.ppermute(one, "dp", [(2, 0), (3, 1), (4, 6), (5, 7)]))
+        any_space = pl.BlockSpec(memory_space=pl.ANY)
+        results = pl.pallas_call(
+            lambda *refs: settle(4, *refs),
+            out_shape=[jax.ShapeDtypeStruct(one.shape, one.dtype) for one in (*whole, *rest)],
+            in_specs=[any_space] * 12,
+            out_specs=[any_space] * 9,
+            scratch_shapes=[
+                pltpu.VMEM((8, *wide[1:]), jnp.bfloat16),
+                pltpu.VMEM((8, *tall[1:]), jnp.bfloat16),
+                pltpu.VMEM((6, *wide[1:]), jnp.float32),
+                pltpu.VMEM((4, *tall[1:]), jnp.float32),
+                dma((4, 8)),
+                dma((4, 8)),
+            ],
+            name="settle",
+            cost_estimate=pl.CostEstimate(flops=10**9, bytes_accessed=141 * 10**6, transcendentals=0),
+            compiler_params=pltpu.CompilerParams(vmem_limit_bytes=62 * 2**20),
+        )(*whole, *hand, *rest)
+        others = []
+        for j in range(3):
+            came[j], _ = lax.optimization_barrier((came[j], results[3]))
+            others.append(lax.ppermute(came[j], "dp", [(0, 1), (1, 0), (6, 7), (7, 6)]))
+
+        def put(which):
+            n = len(which)
+            return pl.pallas_call(
+                lambda *refs: place(n, *refs),
+                out_shape=[jax.ShapeDtypeStruct(results[j].shape, results[j].dtype) for j in which],
+                in_specs=[any_space] * (3 * n),
+                out_specs=[any_space] * n,
+                scratch_shapes=[pltpu.VMEM((2, *hand[j].shape), jnp.bfloat16) for j in which] + [dma((n, 2, LAYERS)), dma((n, 2, LAYERS))],
+                input_output_aliases={i: i for i in range(n)},
+                name="place",
+                cost_estimate=pl.CostEstimate(flops=10**7, bytes_accessed=n * 16 * 10**6, transcendentals=0),
+            )(*(results[j] for j in which), *(came[j] for j in which), *(others[j] for j in which))
+
+        early = put((0, 1))
+        late = put((2,))
+        return (*early, *late, *results[3:])
 
     all_of, cut = P(None, None, None), P(None, "dp", None)
     return jax.shard_map(

time: 732 us -> 694 us (0.948)
  waiting for transfers between devices: 0 us -> 76.6 us
  Pallas kernels: 678 us -> 606 us
  local copies, waits for them, and re-layouts: 52.4 us -> 0.01 us
  starting transfers between devices: 0 us -> 9.96 us
    pallas_call x1, Pallas kernels: 678 us -> 549 us  [step(): pl.pallas_call(lambda *refs: kernel(count, *refs), out_shape=[jax.ShapeDt...]
    ppermute x0 -> x6, waiting for transfers between devices: none -> 76.6 us  [the longest x3 75.6 us: step(): came.append(lax.ppermute(one, 'dp', [(2, 0), (3, 1), (4, 6), (5, 7)]))]
    pallas_call x0 -> x3, Pallas kernels: none -> 57.3 us  [the longest x1 47.9 us: step(): pl.pallas_call(lambda *refs: settle(4, *refs), out_shape=[jax.ShapeDtypeS...]
    unnamed x31 -> x2, local copies, waits for them, and re-layouts: 52.4 us -> 0.01 us
    ppermute x0 -> x6, starting transfers between devices: none -> 9.96 us  [the longest x3 6.08 us: step(): others.append(lax.ppermute(came[j], 'dp', [(0, 1), (1, 0), (6, 7), (7, 6)]))]
  transfers between devices with their start and end apart: 0 -> 6, of which waited for: 0 -> 3; matrix products, arithmetic and copies ran while one was open for 0% -> 0% of each run, Pallas kernels for 0% -> 7%
where the time goes in v2:
time: 694 us; the launch traced here: 693 us
  Pallas kernels  606 us (87%)
  waiting for transfers between devices  76.6 us (11%)
  starting transfers between devices  9.96 us (1%)
    pallas_call x1, Pallas kernels, step(): pl.pallas_call(lambda *refs: kernel(count, *refs), out_shape=[jax.ShapeDt...  549 us
    ppermute x3, waiting for transfers between devices, step(): came.append(lax.ppermute(one, 'dp', [(2, 0), (3, 1), (4, 6), (5, 7)]))  75.6 us
    pallas_call x1, Pallas kernels, step(): pl.pallas_call(lambda *refs: settle(4, *refs), out_shape=[jax.ShapeDtypeS...  47.9 us
  transfers between devices with their start and end apart: 6, of which 3 were waited for; matrix products, arithmetic and copies ran while one was open for 0% of the time, Pallas kernels for 7%

profile of v2, /device:TPU:0, one launch (start us, length us, event | category | flops | bytes accessed | tf_op | source)
XLA Modules:
  0.0 693.3 jit_solution(16901732133371269442)
XLA Ops:
  0.6 548.7 %clipped_step.1 = (bf16[2,1280,3072]{2,1,0:T(8,128)(2,1)}, bf16[2,1280,3072]{2,1,0:T(8,128)(2,1)}, bf16[2,3072,1280]{2,1,0:T(8,128)(2,1)}, bf16[2,160,3072]{2,1,...) custom-call(bf16[2,1280,3072]{2,1,0:T(8,128)(2,1)} %bitcast.3, ...), custom_call_target="tpu_custom_call" | custom-call | tf_op jit(solution)/shard_map/clipped_step/pallas_call | solution.py:483
  549.3 1.3 collective-permute-start.4
  550.6 1.3 collective-permute-start
  551.9 1.3 collective-permute-start.1
  553.2 47.9 %settle.1 = (bf16[2,1280,3072]{2,1,0:T(8,128)(2,1)}, bf16[2,1280,3072]{2,1,0:T(8,128)(2,1)}, bf16[2,3072,1280]{2,1,0:T(8,128)(2,1)}, f32[2,160,3072]{2,1,0:T(8,1...) custom-call(bf16[2,1280,3072]{2,1,0:T(8,128)(2,1)} %get-tuple-elemen, ...), custom_call_target="tpu_custom_call" | custom-call | flops 1000000000 | bytes 141000000 | tf_op jit(solution)/shard_map/settle/pallas_call | solution.py:527
  601.1 0.0 collective-permute-done.4.refs_1_
  601.1 2.3 collective-permute-start.5
  603.4 35.8 %collective-permute-done.refs_2_ = bf16[2,160,3072]{2,1,0:T(8,128)(2,1)S(1)} collective-permute-done((bf16[2,160,3072]{2,1,0:T(8,128)(2,1)}, bf16[2,160,3072]{2,1,0:T(8,128)(2,1)S(1)}, u32[]{:S(2)}, u32[]{:S(2)}) %collective-permute-start) | collective-permute-done | bytes 1966112 | tf_op jit(solution)/shard_map/ppermute | solution.py:525
  639.3 0.0 copy-start
  639.3 1.9 collective-permute-start.2
  641.2 39.7 %collective-permute-done.1.refs_3_ = bf16[2,160,3072]{2,1,0:T(8,128)(2,1)} collective-permute-done((bf16[2,160,3072]{2,1,0:T(8,128)(2,1)}, bf16[2,160,3072]{2,1,0:T(8,128)(2,1)}, u32[]{:S(2)}, u32[]{:S(2)}) %collective-permute-start.1) | collective-permute-done | bytes 1966112 | tf_op jit(solution)/shard_map/ppermute | solution.py:525
  680.9 1.9 collective-permute-start.3
  682.8 0.0 collective-permute-done.5.refs_2_
  682.8 3.2 place.3
  686.0 0.0 copy-done
  686.0 0.0 collective-permute-done.2.refs_4_
  686.0 1.0 collective-permute-done.3.refs_5_
  687.1 6.2 place.2
Async XLA Ops:
  549.3 51.8 %collective-permute-start.4 = (bf16[2,384,1280]{2,1,0:T(8,128)(2,1)}, bf16[2,384,1280]{2,1,0:T(8,128)(2,1)}, u32[]{:S(2)}, u32[]{:S(2)}) collective-permute-start(bf16[2,384,1280]{2,1,0:T(8,128)(2,1)} %get-tuple-element.40.refs_5_), channel_id=1, source_target_pairs={{2,0},{3,1},{4,6},{5,7},{10,8},{11,9},{12,14},{13,15},{18,16},{19,... | collective-permute-start | bytes 5898248 | tf_op jit(solution)/shard_map/ppermute | solution.py:525
  550.6 88.6 %collective-permute-start = (bf16[2,160,3072]{2,1,0:T(8,128)(2,1)}, bf16[2,160,3072]{2,1,0:T(8,128)(2,1)S(1)}, u32[]{:S(2)}, u32[]{:S(2)}) collective-permute-start(bf16[2,160,3072]{2,1,0:T(8,128)(2,1)} %get-tuple-element.38.refs_3_), channel_id=1, source_target_pairs={{2,0},{3,1},{4,6},{5,7},{10,8},{11,9},{12,14},{13,15},{18,16},{19,... | collective-permute-start | bytes 5898248 | tf_op jit(solution)/shard_map/ppermute | solution.py:525
  551.9 129.0 %collective-permute-start.1 = (bf16[2,160,3072]{2,1,0:T(8,128)(2,1)}, bf16[2,160,3072]{2,1,0:T(8,128)(2,1)}, u32[]{:S(2)}, u32[]{:S(2)}) collective-permute-start(bf16[2,160,3072]{2,1,0:T(8,128)(2,1)} %get-tuple-element.39.refs_4_), channel_id=1, source_target_pairs={{2,0},{3,1},{4,6},{5,7},{10,8},{11,9},{12,14},{13,15},{18,16},{19,... | collective-permute-start | bytes 5898248 | tf_op jit(solution)/shard_map/ppermute | solution.py:525
  601.1 81.7 %collective-permute-start.5 = (bf16[2,384,1280]{2,1,0:T(8,128)(2,1)}, bf16[2,384,1280]{2,1,0:T(8,128)(2,1)}, u32[]{:S(2)}, u32[]{:S(2)}) collective-permute-start(bf16[2,384,1280]{2,1,0:T(8,128)(2,1)} %collective-permute-done.4.refs_1_), channel_id=1, source_target_pairs={{0,1},{1,0},{6,7},{7,6},{8,9},{9,8},{14,15},{15,14},{16,17},{17,16... | collective-permute-start | bytes 5898248 | tf_op jit(solution)/shard_map/ppermute | solution.py:547
  639.3 46.8 %copy-start = (bf16[2,160,3072]{2,1,0:T(8,128)(2,1)}, bf16[2,160,3072]{2,1,0:T(8,128)(2,1)S(1)}, u32[]{:S(2)}) copy-start(bf16[2,160,3072]{2,1,0:T(8,128)(2,1)S(1)} %collective-permute-done.refs_2_) | copy-start | bytes 5898244
  639.3 46.8 %collective-permute-start.2 = (bf16[2,160,3072]{2,1,0:T(8,128)(2,1)S(1)}, bf16[2,160,3072]{2,1,0:T(8,128)(2,1)}, u32[]{:S(2)}, u32[]{:S(2)}) collective-permute-start(bf16[2,160,3072]{2,1,0:T(8,128)(2,1)S(1)} %collective-permute-done.refs_2_), channel_id=1, source_target_pairs={{0,1},{1,0},{6,7},{7,6},{8,9},{9,8},{14,15},{15,14},{16,17},{17,16... | collective-permute-start | bytes 5898248 | tf_op jit(solution)/shard_map/ppermute | solution.py:547
  680.9 6.2 collective-permute-start.3
